TPU v7x, 128 devices: a whole 4x4x4 slice. The times are simulated.
128 devices in a mesh: dp: 1, cp: 128 (over z, y, x, core).
Axes of the slice: x: 4, y: 4, z: 4, core: 2. Of those that a mesh axis runs over, the one named last changes fastest.
Arguments:
- queries: bfloat16 [3072, 28, 128], P(('dp', 'cp'))
- key_new: bfloat16 [3072, 4, 128], P(('dp', 'cp'))
- value_new: bfloat16 [3072, 4, 128], P(('dp', 'cp'))
- key_cache: bfloat16 [196608, 4, 128], P(('dp', 'cp'))
- value_cache: bfloat16 [196608, 4, 128], P(('dp', 'cp'))
- prefix_len: int32 [1], P('dp')
Outputs:
- output 1: bfloat16 [3072, 28, 128], P(('dp', 'cp'))
- output 2: float32 [3072, 28], P(('dp', 'cp'))
All inputs are finite; a program needn't handle non-finite values.
Results may differ from a plain program's by a relative error of at most 0.00749064.
Values are sent between devices in bfloat16 or wider.
A program may use at most 1 GiB of HBM per device.

v0:
```python
import jax
import jax.numpy as jnp
from jax import lax
from jax.sharding import PartitionSpec as P

MASK_FILL = -1e30


def solution(mesh):
    groups = mesh.shape['cp']
    send_pairs = [(src_idx, (src_idx + 1) % groups) for src_idx in range(groups)]
    tok_spec = P(('dp', 'cp'))

    def local_attend(queries, key_new, value_new, key_cache, value_cache, prefix_len):
        tok_rows, num_heads, head_dim = queries.shape
        cache_len, kv_heads = key_cache.shape[0], key_cache.shape[1]
        group_ratio = num_heads // kv_heads
        logit_scale = head_dim ** -0.5
        my_rank = lax.axis_index('cp')
        cache_seen = my_rank * cache_len + jnp.arange(cache_len) < prefix_len[0]
        row_ids = jnp.arange(tok_rows)
        key_ids = my_rank * tok_rows + row_ids

        def absorb(loop_step, q_blk, out_acc, row_max, row_sum):
            source = (my_rank - loop_step) % groups
            q_grouped = q_blk.reshape(tok_rows, kv_heads, group_ratio, head_dim)
            s_cache = jnp.einsum('tkgd,skd->kgts', q_grouped, key_cache, preferred_element_type=jnp.float32) * logit_scale
            s_cache = jnp.where(cache_seen, s_cache, MASK_FILL)
            s_fresh = jnp.einsum('tkgd,skd->kgts', q_grouped, key_new, preferred_element_type=jnp.float32) * logit_scale
            fresh_seen = key_ids[None, :] <= (source * tok_rows + row_ids)[:, None]
            s_fresh = jnp.where(fresh_seen, s_fresh, MASK_FILL)
            next_max = jnp.maximum(row_max, jnp.maximum(s_cache.max(axis=-1), s_fresh.max(axis=-1)))
            e_cache = jnp.exp(s_cache - next_max[..., None])
            e_fresh = jnp.exp(s_fresh - next_max[..., None])
            rescale_by = jnp.exp(row_max - next_max)
            row_sum = row_sum * rescale_by + e_cache.sum(axis=-1) + e_fresh.sum(axis=-1)
            out_acc = (out_acc * rescale_by[..., None]
                       + jnp.einsum('kgts,skd->kgtd', e_cache.astype(jnp.bfloat16), value_cache, preferred_element_type=jnp.float32)
                       + jnp.einsum('kgts,skd->kgtd', e_fresh.astype(jnp.bfloat16), value_new, preferred_element_type=jnp.float32))
            return out_acc, next_max, row_sum

        def one_step(loop_step, state):
            q_blk, out_acc, row_max, row_sum = state
            out_acc, row_max, row_sum = absorb(loop_step, q_blk, out_acc, row_max, row_sum)
            return lax.ppermute((q_blk, out_acc, row_max, row_sum), 'cp', send_pairs)

        start_acc = jnp.zeros((kv_heads, group_ratio, tok_rows, head_dim), jnp.float32)
        start_max = jnp.full((kv_heads, group_ratio, tok_rows), MASK_FILL, jnp.float32)
        start_sum = jnp.zeros((kv_heads, group_ratio, tok_rows), jnp.float32)
        q_blk, out_acc, row_max, row_sum = lax.fori_loop(0, groups - 1, one_step, (queries, start_acc, start_max, start_sum))
        out_acc, row_max, row_sum = absorb(groups - 1, q_blk, out_acc, row_max, row_sum)
        out_acc, row_max, row_sum = lax.ppermute((out_acc, row_max, row_sum), 'cp', send_pairs)
        attn_out = (out_acc / row_sum[..., None]).transpose(2, 0, 1, 3).reshape(tok_rows, num_heads, head_dim).astype(jnp.bfloat16)
        row_lse = (row_max + jnp.log(row_sum)).transpose(2, 0, 1).reshape(tok_rows, num_heads)
        return attn_out, row_lse

    return jax.shard_map(local_attend, mesh=mesh, in_specs=(tok_spec, tok_spec, tok_spec, tok_spec, tok_spec, P('dp')), out_specs=(tok_spec, tok_spec), check_vma=False)
```

profile of v0, /device:TPU:0, one launch (start us, length us, event | category | flops | bytes accessed | tf_op | source)
XLA Modules:
  0.0 2843.5 jit_solution(16625692578141642373)
XLA Ops:
  6.1 2815.9 %while.22 = (s32[]{:T(128)}, bf16[24,28,128]{2,0,1:T(8,128)(2,1)S(1)}, f32[4,7,24,128]{3,2,1,0:T(8,128)}, f32[4,7,24]{2,1,0:T(8,128)S(1)}, f32[4,7,24]{2,1,0:T(8...) while((s32[]{:T(128)}, ...), condition=%wide.region_5.6_spmd.clone, body=%wide.region_0.5_spmd.clone.sunk | while | flops 544341184 | bytes 20082164 | solution.py:50
  37.3 14.0 collective-permute-done.2
  59.5 14.0 collective-permute-done.2
  81.7 14.0 collective-permute-done.2
  103.8 14.0 collective-permute-done.2
  126.0 14.0 collective-permute-done.2
  148.2 14.0 collective-permute-done.2
  170.3 14.0 collective-permute-done.2
  192.5 14.0 collective-permute-done.2
  214.7 14.0 collective-permute-done.2
  236.8 14.0 collective-permute-done.2
  259.0 14.0 collective-permute-done.2
  281.2 14.0 collective-permute-done.2
  303.3 14.0 collective-permute-done.2
  325.5 14.0 collective-permute-done.2
  347.6 14.0 collective-permute-done.2
  392.0 14.0 collective-permute-done.2
  414.1 14.0 collective-permute-done.2
  436.3 14.0 collective-permute-done.2
  458.5 14.0 collective-permute-done.2
  480.6 14.0 collective-permute-done.2
  502.8 14.0 collective-permute-done.2
  525.0 14.0 collective-permute-done.2
  547.1 14.0 collective-permute-done.2
  569.3 14.0 collective-permute-done.2
  591.5 14.0 collective-permute-done.2
  613.6 14.0 collective-permute-done.2
  635.8 14.0 collective-permute-done.2
  657.9 14.0 collective-permute-done.2
  680.1 14.0 collective-permute-done.2
  702.3 14.0 collective-permute-done.2
  724.4 14.0 collective-permute-done.2
  (2930 shorter events, 2395.3 us)
Async XLA Ops:
  14.0 15.4 collective-permute-start.1
  14.0 15.4 collective-permute-start
  37.2 14.3 collective-permute-start.1
  59.4 14.3 collective-permute-start.1
  81.6 14.3 collective-permute-start.1
  125.9 14.3 collective-permute-start.1
  170.2 14.3 collective-permute-start.1
  192.4 14.3 collective-permute-start.1
  214.6 14.3 collective-permute-start.1
  236.7 14.3 collective-permute-start.1
  258.9 14.3 collective-permute-start.1
  281.0 14.3 collective-permute-start.1
  303.2 14.3 collective-permute-start.1
  325.4 14.3 collective-permute-start.1
  347.5 14.3 collective-permute-start.1
  369.7 14.3 collective-permute-start.1
  391.9 14.3 collective-permute-start.1
  414.0 14.3 collective-permute-start.1
  458.4 14.3 collective-permute-start.1
  502.7 14.3 collective-permute-start.1
  547.0 14.3 collective-permute-start.1
  591.3 14.3 collective-permute-start.1
  613.5 14.3 collective-permute-start.1
  635.7 14.3 collective-permute-start.1
  657.8 14.3 collective-permute-start.1
  680.0 14.3 collective-permute-start.1
  702.2 14.3 collective-permute-start.1
  724.3 14.3 collective-permute-start.1
  746.5 14.3 collective-permute-start.1
  768.7 14.3 collective-permute-start.1
  790.8 14.3 collective-permute-start.1
  813.0 14.3 collective-permute-start.1
  (612 other events, 7281.5 us)
where the time goes:
time: 2860 us; the launch traced here: 2840 us
  waiting for transfers between devices  1810 us (63%)
  matrix products  624 us (22%)
  other arithmetic  370 us (13%)
    ppermute x508, waiting for transfers between devices, one_step(): return lax.ppermute((q_blk, out_acc, row_max, row_sum), 'cp', send_pairs)  1800 us
    dot_general x128, matrix products, absorb(): jnp.einsum('kgts,skd->kgtd', e_cache.astype(jnp.bfloat16), value_cache, p...  275 us
    add x128, other arithmetic, absorb(): row_sum = row_sum * rescale_by + e_cache.sum(axis=-1) + e_fresh.sum(axis=-1)  171 us
    dot_general x128, matrix products, absorb(): jnp.einsum('tkgd,skd->kgts', q_grouped, key_cache, preferred_element_type...  165 us
    dot_general x128, matrix products, absorb(): jnp.einsum('kgts,skd->kgtd', e_fresh.astype(jnp.bfloat16), value_new, pre...  131 us
    reduce_sum x256, other arithmetic, absorb(): row_sum = row_sum * rescale_by + e_cache.sum(axis=-1) + e_fresh.sum(axis=-1)  104 us
    lt x128, other arithmetic, local_attend(): cache_seen = my_rank * cache_len + jnp.arange(cache_len) < prefix_len[0]  83.1 us
  transfers between devices with their start and end apart: 511, of which 256 were waited for; matrix products, arithmetic and copies ran while one was open for 0% of the time, Pallas kernels for 0%

commit v1 on v0

v1 whole, which is shorter than its diff:
```python
import functools
import math

import jax
import jax.numpy as jnp
from jax import lax
from jax.experimental import pallas as pl
from jax.experimental.pallas import tpu as pltpu
from jax.sharding import PartitionSpec as P

ZD, YD, XD = 4, 4, 4
SIM = True

HEADS, KV, HD = 28, 4, 128
RATIO = HEADS // KV
FILL = -1e30
SCALE2 = HD ** -0.5 * math.log2(math.e)
LN2 = math.log(2.0)
PAD = 32
BF, F32 = jnp.bfloat16, jnp.float32


def ring_offsets():
    def hops(d, n):
        return min(d, n - d)

    offs = [(dy, dz) for dz in range(ZD) for dy in range(YD)]
    return sorted(offs, key=lambda o: (hops(o[0], YD) + hops(o[1], ZD), o[1], o[0]))


class Mxu:
    def __init__(self, accs):
        self.acc = accs
        self.staged = [[None, None], [None, None]]
        self.loaded = [None, None]
        self.val = [[None] * 4, [None] * 4]

    def push(self, rhs, reg, t):
        if not SIM:
            pltpu.matmul_push_rhs(rhs, reg, t)
        else:
            self.staged[t][reg] = rhs

    def mul(self, t, a, lhs, reg):
        if not SIM:
            pltpu.matmul_acc_lhs(self.acc[t][a], lhs, load_staged_rhs=reg)
        else:
            r = jnp.dot(lhs, self.staged[t][reg], preferred_element_type=F32)
            self.val[t][a] = r if self.val[t][a] is None else self.val[t][a] + r

    def pop(self, t, a):
        if not SIM:
            return pltpu.matmul_pop(self.acc[t][a])
        r, self.val[t][a] = self.val[t][a], None
        return r


def make_kernel(tok, cache):
    offs = ring_offsets()
    G = len(offs)
    PIECE = RATIO * tok
    UNIT = XD * PIECE
    ROWS = G * UNIT
    NPAIR = -(-ROWS // 512)
    CHB = 2 * cache // 256
    NCB = XD * CHB
    NKB = NCB + 1
    LSE_ROWS = UNIT // 128 + 1
    assert cache % 256 == 0 and 8 * PAD == 256 and tok <= PAD

    def kernel(plen, q_in, k_in, v_in, n_in, tq_in, out, lse_out,
               kb, vb, bias, qx, qall, qt, sb, oacc, mb, lb, mcur, tq, keyid, nrecv,
               obuf, lbuf, orecv, lrecv, fo, fl,
               lsem, q_ss, q_rs, b_ss, b_rs, k_ss, k_rs, f_ss, n_ss, n_rs,
               o_ss, o_rs, l_ss, l_rs, x_ss, x_rs, y_ss, y_rs):
        cp = lax.axis_index("cp")
        c = cp % 2
        x = (cp // 2) % XD
        y = (cp // (2 * XD)) % YD
        z = cp // (2 * XD * YD)
        row0 = (z * YD + y) * XD

        def at(xx, yy, zz, cc):
            return ((zz * YD + yy) * XD + xx) * 2 + cc

        def x_peer(dd):
            return at((x + dd) % XD, y, z, c)

        mate = at(x, y, z, 1 - c)

        def to_peer(w):
            dy, dz = offs[w]
            return at(x, (y + dy) % YD, (z + dz) % ZD, c)

        def from_peer(w):
            dy, dz = offs[w]
            return at(x, (y + YD - dy) % YD, (z + ZD - dz) % ZD, c)

        def rc(src, dst, ss, rs, dev):
            return pltpu.make_async_remote_copy(
                src_ref=src, dst_ref=dst, send_sem=ss, recv_sem=rs,
                device_id={"cp": dev}, device_id_type=pl.DeviceIdType.MESH)

        row_devs = [(dd, dc) for dd in range(XD) for dc in range(2) if (dd, dc) != (0, 0)]

        def row_peer(dd, dc):
            return at((x + dd) % XD, y, z, (c + dc) % 2)

        barrier = pltpu.get_barrier_semaphore()
        peers = [to_peer(w) for w in range(1, G)] + [row_peer(dd, dc) for dd, dc in row_devs]
        for p in peers:
            pl.semaphore_signal(barrier, inc=1, device_id={"cp": p}, device_id_type=pl.DeviceIdType.MESH)
        me_j = x * 2 + c
        local = [
            pltpu.make_async_copy(q_in.at[x], qx.at[x], lsem.at[0]),
            pltpu.make_async_copy(k_in.at[x], kb.at[pl.ds(c * cache, cache)], lsem.at[1]),
            pltpu.make_async_copy(v_in.at[x], vb.at[pl.ds(c * cache, cache)], lsem.at[2]),
            pltpu.make_async_copy(n_in.at[x], nrecv.at[me_j], lsem.at[3]),
            pltpu.make_async_copy(tq_in, tq, lsem.at[4]),
        ]
        for cpy in local:
            cpy.start()

        prefix = plen[0]
        riota = lax.broadcasted_iota(jnp.int32, (256, 128), 0)
        lane0 = lax.broadcasted_iota(jnp.int32, (256, 128), 1) == 0
        nblk = cache // 256

        def bias_block(b, _):
            slot = b // nblk
            base = ((row0 + (x + slot // 2) % XD) * 2 + slot % 2) * cache + (b % nblk) * 256
            hide = jnp.where(lane0 & (riota + base >= prefix), FILL, 0.0)
            bias[pl.ds(pl.multiple_of(b * 256, 256), 256), :] = hide.astype(BF)
            return 0

        lax.fori_loop(0, NCB, bias_block, 0)
        bias[pl.ds(NCB * 256, 256), :] = jnp.zeros((256, 128), BF)
        dev_j = lax.shift_right_logical(riota, 5)
        r_j = lax.bitwise_and(riota, PAD - 1)
        keyid[...] = jnp.where(r_j < tok, (row0 * 2 + dev_j) * tok + r_j, 1 << 23).astype(F32)

        pl.semaphore_wait(barrier, len(peers))

        q_send = [rc(q_in.at[(x + dd) % XD], qx.at[x], q_ss.at[dd], q_rs.at[x], x_peer(dd)) for dd in range(1, XD)]
        for cpy in q_send:
            cpy.start()
        own = pl.ds(c * cache, cache)
        kv_send = [rc(k_in.at[x], kb.at[own], k_ss.at[0, 0], k_rs.at[c, 0], mate),
                   rc(v_in.at[x], vb.at[own], k_ss.at[0, 1], k_rs.at[c, 1], mate)]
        order = [1, XD - 1] + [d for d in range(2, XD - 1)]
        for dd in order:
            slot = ((XD - dd) % XD) * 2 + c
            there = pl.ds(slot * cache, cache)
            kv_send.append(rc(k_in.at[(x + dd) % XD], kb.at[there], k_ss.at[dd, 0], k_rs.at[slot, 0], x_peer(dd)))
            kv_send.append(rc(v_in.at[(x + dd) % XD], vb.at[there], k_ss.at[dd, 1], k_rs.at[slot, 1], x_peer(dd)))
        for cpy in kv_send:
            cpy.start()
        n_send = [rc(n_in.at[(x + dd) % XD], nrecv.at[me_j], n_ss.at[i], n_rs.at[me_j], row_peer(dd, dc))
                  for i, (dd, dc) in enumerate(row_devs)]
        for cpy in n_send:
            cpy.start()

        local[0].wait()
        for dd in range(1, XD):
            src = (x + dd) % XD
            rc(q_in.at[x], qx.at[src], q_ss.at[dd], q_rs.at[src], x_peer(dd)).wait_recv()
        own_rows = jnp.concatenate([qx[i].astype(F32) for i in range(XD)], axis=0).astype(BF)
        qall[pl.ds(0, UNIT), :] = own_rows
        b_send = [rc(qall.at[pl.ds(0, UNIT)], qall.at[pl.ds(w * UNIT, UNIT)], b_ss.at[w], b_rs.at[w], from_peer(w))
                  for w in range(1, G)]
        for cpy in b_send:
            cpy.start()

        def wait_unit(w):
            there = pl.ds(pl.multiple_of(w * UNIT, 16), UNIT)
            rc(qall.at[pl.ds(0, UNIT)], qall.at[there], b_ss.at[w], b_rs.at[w], mate).wait_recv()

        def units_for(p):
            return jnp.minimum((p * 512 + 511) // UNIT + 1, G)

        def prep(p):
            for t in range(2):
                rows = qall[pl.ds(pl.multiple_of((p * 2 + t) * 256, 256), 256), :]
                qt[p * 2 + t] = rows.T

        ones_row = jnp.where(lax.broadcasted_iota(jnp.int32, (128, 256), 0) == 0, 1.0, 0.0).astype(BF)

        def rep(v, n):
            return jnp.concatenate([v] * n, axis=0)

        def unit_body(mx, blocks, pv, qk, first, prep_pair):
            if prep_pair is not None:
                prep(prep_pair)
            n = len(blocks)
            if pv is not None:
                mp = [mcur[t] for t in range(2)]
                lacc = [jnp.zeros((8, 256), F32) for _ in range(2)]
            if qk is not None:
                mxs = [jnp.full((8, 256), -jnp.inf, F32) for _ in range(2)]

                def qpush(t):
                    mx.push(jnp.concatenate([qt[qk * 2 + t], ones_row], axis=0), 0, t)

                for t in range(2):
                    qpush(t)
            for i, b in enumerate(blocks):
                if qk is not None:
                    k = jnp.concatenate([kb[pl.ds(b * 256, 256), :], bias[pl.ds(b * 256, 256), :]], axis=1)
                    for t in range(2):
                        mx.mul(t, i % 3, k, 0)
                if pv is not None:
                    for t in range(2):
                        p = jnp.exp2((sb[t, i] - rep(mp[t], 32)) * SCALE2)
                        lacc[t] = lacc[t] + p.reshape(32, 8, 256).sum(0)
                        mx.push(p.astype(BF), 1, t)
                    vt = jnp.concatenate([vb[pl.ds(b * 256, 128), :], vb[pl.ds(b * 256 + 128, 128), :]], axis=1)
                    for t in range(2):
                        mx.mul(t, 3, vt, 1)
                if qk is not None:
                    if i < n - 1:
                        for t in range(2):
                            qpush(t)
                    for t in range(2):
                        s = mx.pop(t, i % 3)
                        if b == NCB:
                            lim = rep(tq[qk * 2 + t], 32)
                            kid = jnp.concatenate([keyid[...], keyid[...]], axis=1)
                            s = jnp.where(kid <= lim, s, FILL)
                        sb[t, i] = s
                        mxs[t] = jnp.maximum(mxs[t], s.reshape(32, 8, 256).max(0))
            if pv is not None:
                for t in range(2):
                    o = mx.pop(t, 3)
                    tile = pv * 2 + t
                    if first:
                        oacc[tile] = o
                        lb[tile] = lacc[t]
                    else:
                        alpha = jnp.exp2((mb[tile] - mp[t]) * SCALE2)
                        l = jnp.sum(lacc[t] + alpha * lb[tile], axis=0, keepdims=True)
                        inv = 1.0 / l
                        o = (oacc[tile] * rep(alpha, 16) + o) * inv
                        obuf[pl.ds(pl.multiple_of(tile * 256, 256), 256), :] = o.T.astype(BF)
                        ls = mp[t][0:1] * SCALE2 + jnp.log2(l)
                        lbuf[tile * 2] = ls[:, 0:128]
                        lbuf[tile * 2 + 1] = ls[:, 128:256]
            if qk is not None:
                for t in range(2):
                    m = jnp.broadcast_to(jnp.max(mxs[t], axis=0, keepdims=True), (8, 256))
                    if first:
                        mb[qk * 2 + t] = m
                    else:
                        m = jnp.maximum(m, mb[qk * 2 + t])
                    mcur[t] = m

        def compute(*accs):
            mx = Mxu([accs[:4], accs[4:]])

            for cpy in local[1:]:
                cpy.wait()
            other = pl.ds((1 - c) * cache, cache)
            rc(k_in.at[x], kb.at[other], k_ss.at[0, 0], k_rs.at[1 - c, 0], mate).wait_recv()
            rc(v_in.at[x], vb.at[other], k_ss.at[0, 1], k_rs.at[1 - c, 1], mate).wait_recv()
            u_first = int(units_for_py(min(1, NPAIR - 1)))
            for w in range(1, u_first):
                wait_unit(w)
            blocks = list(range(CHB))
            prep(0)
            unit_body(mx, blocks, None, 0, True, 1 if NPAIR > 1 else None)

            def forward(dxs):
                for dx in dxs:
                    mine = pl.ds((dx * 2 + c) * cache, cache)
                    for kv, buf in enumerate((kb, vb)):
                        rc(buf.at[mine], buf.at[mine], f_ss.at[dx, kv], k_rs.at[dx * 2 + c, kv], mate).wait_recv()
                        rc(buf.at[mine], buf.at[mine], f_ss.at[dx, kv], k_rs.at[dx * 2 + c, kv], mate).start()

            near = sorted({1, XD - 1})
            far = [d for d in range(1, XD) if d not in near]
            u_near = min(15, max(NPAIR - 3, 0))

            def pass_a(u, _):
                have, need = units_for(u + 1), units_for(u + 2)

                @pl.when(need > have)
                def _():
                    wait_unit(have)

                @pl.when(u == u_near)
                def _():
                    forward(near)

                unit_body(mx, blocks, u, u + 1, True, jnp.minimum(u + 2, NPAIR - 1))
                return 0

            lax.fori_loop(0, NPAIR - 1, pass_a, 0)
            unit_body(mx, blocks, NPAIR - 1, None, True, None)

            forward(far)
            for i in range(1, 8):
                j = (me_j + i) % 8
                rc(n_in.at[x], nrecv.at[j], n_ss.at[0], n_rs.at[j], mate).wait_recv()
            newk = jnp.concatenate([nrecv[j, 0] for j in range(8)], axis=0)
            newv = jnp.concatenate([nrecv[j, 1] for j in range(8)], axis=0).T
            kb[pl.ds(NCB * 256, 256), :] = newk
            vb[pl.ds(NCB * 256, 128), :] = newv[:, 0:128]
            vb[pl.ds(NCB * 256 + 128, 128), :] = newv[:, 128:256]
            for dx in range(1, XD):
                theirs = pl.ds((dx * 2 + 1 - c) * cache, cache)
                for kv, buf in enumerate((kb, vb)):
                    rc(buf.at[theirs], buf.at[theirs], f_ss.at[dx, kv], k_rs.at[dx * 2 + 1 - c, kv], mate).wait_recv()
            blocks_b = list(range(CHB, NKB))
            unit_body(mx, blocks_b, None, NPAIR - 1, False, None)

            def send_unit(p):
                for w in range(1, G):
                    @pl.when(p == (w * UNIT) // 512)
                    def _():
                        for cpy in out_copies(w):
                            cpy.start()

            def pass_b(u, _):
                p = NPAIR - 1 - u
                unit_body(mx, blocks_b, p, p - 1, False, None)
                send_unit(p)
                return 0

            lax.fori_loop(0, NPAIR - 1, pass_b, 0)
            unit_body(mx, blocks_b, 0, None, False, None)
            send_unit(jnp.int32(0))

        def units_for_py(p):
            return min((p * 512 + 511) // UNIT + 1, G)

        def out_copies(w):
            e0 = (w * UNIT) // 128
            return [rc(obuf.at[pl.ds(w * UNIT, UNIT)], orecv.at[w], o_ss.at[w], o_rs.at[w], to_peer(w)),
                    rc(lbuf.at[pl.ds(e0, LSE_ROWS)], lrecv.at[w], l_ss.at[w], l_rs.at[w], to_peer(w))]

        if SIM:
            compute(*([None] * 8))
        else:
            pl.run_scoped(compute, *[pltpu.ACC(t)((128 if a == 3 else 256, 256), F32)
                                     for t in range(2) for a in range(4)])

        for w in range(1, G):
            rc(obuf.at[pl.ds(0, UNIT)], orecv.at[w], o_ss.at[w], o_rs.at[w], mate).wait_recv()
            rc(lbuf.at[pl.ds(0, LSE_ROWS)], lrecv.at[w], l_ss.at[w], l_rs.at[w], mate).wait_recv()
        lane = lax.broadcasted_iota(jnp.int32, (LSE_ROWS, 128), 1)

        def shifted(v, off):
            if off == 0:
                return v
            r = pltpu.roll(v, 128 - off, 1)
            nxt = jnp.concatenate([r[1:], r[-1:]], axis=0)
            return jnp.where(lane[: v.shape[0]] < 128 - off, r, nxt)

        def lse_of(w):
            v = lbuf[pl.ds(0, LSE_ROWS)] if w == 0 else lrecv[w]
            return shifted(v.reshape(LSE_ROWS, 128), (w * UNIT) % 128)

        lses = [lse_of(w) for w in range(G)]
        top = functools.reduce(jnp.maximum, lses)
        wts = [jnp.exp2(v - top) for v in lses]
        den = functools.reduce(jnp.add, wts)
        inv = 1.0 / den
        wts = [v * inv for v in wts]
        total = (top + jnp.log2(den)) * LN2
        pieces = []
        for j in range(-(-UNIT // 128)):
            n = min(128, UNIT - j * 128)
            cols = jnp.concatenate([v[j:j + 1] for v in wts] + [jnp.zeros((128 - G, 128), F32)], axis=0).T
            acc = jnp.zeros((n, 128), F32)
            for w in range(G):
                src = obuf[pl.ds(j * 128, n), :] if w == 0 else orecv[w, pl.ds(j * 128, n), :]
                acc = acc + src.astype(F32) * cols[:n, w:w + 1]
            pieces.append(acc)
        final = jnp.concatenate(pieces, axis=0)
        for i in range(XD):
            fo[i] = final[i * PIECE:(i + 1) * PIECE].astype(BF)
            off = (i * PIECE) % 128
            e = (i * PIECE) // 128
            need = min(3, LSE_ROWS - e)
            v = shifted(total[e:e + need], off)
            v = v if need >= 2 else jnp.concatenate([v, v], axis=0)
            fl[2 * i] = v[0:1]
            fl[2 * i + 1] = v[1:2]
        x_send = []
        for dd in range(1, XD):
            xd = (x + dd) % XD
            x_send.append(rc(fo.at[xd], out.at[x], x_ss.at[dd], x_rs.at[x], x_peer(dd)))
            x_send.append(rc(fl.at[pl.ds(2 * xd, 2)], lse_out.at[pl.ds(2 * x, 2)], y_ss.at[dd], y_rs.at[x], x_peer(dd)))
        for cpy in x_send:
            cpy.start()
        mine = [pltpu.make_async_copy(fo.at[x], out.at[x], lsem.at[0]),
                pltpu.make_async_copy(fl.at[pl.ds(2 * x, 2)], lse_out.at[pl.ds(2 * x, 2)], lsem.at[1])]
        for cpy in mine:
            cpy.start()
        for cpy in q_send + kv_send + n_send + b_send + x_send:
            cpy.wait_send()
        for dx in range(1, XD):
            m = pl.ds((dx * 2 + c) * cache, cache)
            for kv, buf in enumerate((kb, vb)):
                rc(buf.at[m], buf.at[m], f_ss.at[dx, kv], k_rs.at[dx * 2 + c, kv], mate).wait_send()
        for w in range(1, G):
            for cpy in out_copies(w):
                cpy.wait_send()
        for cpy in mine:
            cpy.wait()
        for dd in range(1, XD):
            src = (x + dd) % XD
            rc(fo.at[0], out.at[src], x_ss.at[dd], x_rs.at[src], x_peer(dd)).wait_recv()
            rc(fl.at[pl.ds(0, 2)], lse_out.at[pl.ds(2 * src, 2)], y_ss.at[dd], y_rs.at[src], x_peer(dd)).wait_recv()

    D, R = pltpu.SemaphoreType.DMA, NPAIR * 2
    V = pltpu.VMEM
    scratch = [
        V((NKB * 256, 128), BF), V((NKB * 256, 128), BF), V((NKB * 256, 128), BF),
        V((XD, PIECE, 128), BF), V((NPAIR * 512, 128), BF), V((R, 128, 256), BF),
        V((2, NKB - CHB, 256, 256), F32), V((R, 128, 256), F32),
        V((R, 8, 256), F32), V((R, 8, 256), F32), V((2, 8, 256), F32), V((R, 8, 256), F32),
        V((256, 128), F32), V((8, 2, PAD, 128), BF),
        V((NPAIR * 512, 128), BF), V((R * 2 + LSE_ROWS, 1, 128), F32),
        V((G, UNIT, 128), BF), V((G, LSE_ROWS, 1, 128), F32),
        V((XD, PIECE, 128), BF), V((2 * XD, 1, 128), F32),
        D((5,)), D((XD,)), D((XD,)), D((G,)), D((G,)), D((XD, 2)), D((2 * XD, 2)), D((XD, 2)), D((7,)), D((8,)),
        D((G,)), D((G,)), D((G,)), D((G,)), D((XD,)), D((XD,)), D((XD,)), D((XD,)),
    ]
    any_ = pl.BlockSpec(memory_space=pl.ANY)
    return pl.pallas_call(
        kernel,
        out_shape=(jax.ShapeDtypeStruct((XD, PIECE, 128), BF), jax.ShapeDtypeStruct((2 * XD, 1, 128), F32)),
        in_specs=[pl.BlockSpec(memory_space=pltpu.SMEM)] + [any_] * 5,
        out_specs=(any_, any_),
        scratch_shapes=scratch,
        name="prefix_attention",
        compiler_params=pltpu.CompilerParams(collective_id=0, has_side_effects=True, vmem_limit_bytes=63 << 20),
    ), (offs, G, PIECE, UNIT, ROWS, NPAIR)


def solution(mesh):
    spec = P(("dp", "cp"))

    def local(queries, key_new, value_new, key_cache, value_cache, prefix_len):
        tok, cache = queries.shape[0], key_cache.shape[0]
        call, (offs, G, PIECE, UNIT, ROWS, NPAIR) = make_kernel(tok, cache)
        cp = lax.axis_index("cp")
        c, y, z = cp % 2, (cp // (2 * XD)) % YD, cp // (2 * XD * YD)
        q = queries.transpose(1, 0, 2).reshape(KV, PIECE, HD)
        k = key_cache.transpose(1, 0, 2)
        v = value_cache.reshape(cache // 128, 128, KV, HD).transpose(2, 0, 3, 1).reshape(KV, cache, 128)
        new = jnp.stack([key_new.transpose(1, 0, 2), value_new.transpose(1, 0, 2)], axis=1)
        new = jnp.pad(new, ((0, 0), (0, 0), (0, PAD - tok), (0, 0)))
        dy = jnp.array([o[0] for o in offs], jnp.int32)
        dz = jnp.array([o[1] for o in offs], jnp.int32)
        chip_row = (((z + dz) % ZD) * YD + (y + dy) % YD) * XD
        dev = (chip_row[:, None] + jnp.arange(XD)[None, :]) * 2 + c
        token = dev[:, :, None, None] * tok + jnp.arange(tok)[None, None, None, :]
        token = jnp.broadcast_to(token, (G, XD, RATIO, tok)).reshape(ROWS)
        token = jnp.pad(token, (0, NPAIR * 512 - ROWS)).astype(F32)
        tq = jnp.broadcast_to(token.reshape(NPAIR * 2, 1, 256), (NPAIR * 2, 8, 256))
        out, lse = call(prefix_len, q, k, v, new, tq)
        attn_out = out.reshape(HEADS, tok, HD).transpose(1, 0, 2)
        row_lse = lse.reshape(KV, 256)[:, :PIECE].reshape(HEADS, tok).T
        return attn_out, row_lse

    return jax.shard_map(local, mesh=mesh, in_specs=(spec,) * 5 + (P("dp"),), out_specs=(spec, spec), check_vma=False)
```

time: 2860 us -> 188 us (0.07)
  waiting for transfers between devices: 1810 us -> 0 us
  matrix products: 624 us -> 0 us
  other arithmetic: 370 us -> 2.83 us
  Pallas kernels: 0 us -> 173 us
    ppermute x511 -> x0, waiting for transfers between devices: 1810 us -> none  [the longest x508 1800 us: one_step(): return lax.ppermute((q_blk, out_acc, row_max, row_sum), 'cp', send_pairs)]
    dot_general x512 -> x0, matrix products: 624 us -> none  [the longest x128 275 us: absorb(): jnp.einsum('kgts,skd->kgtd', e_cache.astype(jnp.bfloat16), value_cache, p...]
    pallas_call x0 -> x1, Pallas kernels: none -> 173 us  [local(): out, lse = call(prefix_len, q, k, v, new, tq)]
    add x383 -> x0, other arithmetic: 172 us -> none  [the longest x128 171 us: absorb(): row_sum = row_sum * rescale_by + e_cache.sum(axis=-1) + e_fresh.sum(axis=-1)]
    reduce_sum x256 -> x0, other arithmetic: 104 us -> none  [absorb(): row_sum = row_sum * rescale_by + e_cache.sum(axis=-1) + e_fresh.sum(axis=-1)]
    lt x128 -> x0, other arithmetic: 83.1 us -> none  [local_attend(): cache_seen = my_rank * cache_len + jnp.arange(cache_len) < prefix_len[0]]
  transfers between devices with their start and end apart: 511 -> 0, of which waited for: 256 -> 0; matrix products, arithmetic and copies ran while one was open for 0% -> 0% of each run, Pallas kernels for 0% -> 0%
where the time goes in v1:
time: 188 us; the launch traced here: 186 us
  Pallas kernels  173 us (92%)
  local copies, waits for them, and re-layouts  9.72 us (5%)
  other arithmetic  2.83 us (2%)
    pallas_call x1, Pallas kernels, local(): out, lse = call(prefix_len, q, k, v, new, tq)  173 us
    unnamed x5, local copies, waits for them, and re-layouts  5.18 us

profile of v1, /device:TPU:0, one launch (start us, length us, event | category | flops | bytes accessed | tf_op | source)
XLA Modules:
  0.0 186.4 jit_solution(5610566778229502816)
XLA Ops:
  0.7 0.7 fusion.7
  1.4 0.1 add_multiply_fusion
  1.4 0.1 add_convert_fusion
  1.6 0.1 convert_element_type.14
  1.7 0.8 broadcast_in_dim.5.tq_in
  2.5 0.8 copy_bitcast_fusion.1
  3.2 0.6 fusion.2.n_in
  3.9 0.0 copy-start
  3.9 2.9 %copy.22 = bf16[1536,4,128]{2,0,1:T(8,128)(2,1)} copy(bf16[1536,4,128]{2,1,0:T(4,128)(2,1)} %param.11) | data formatting | bytes 3145728 | tf_op args[3]
  6.8 0.0 copy-done
  6.8 2.3 %copy.15 = bf16[12,128,4,128]{1,3,0,2:T(8,128)(2,1)} copy(bf16[12,128,4,128]{3,2,1,0:T(4,128)(2,1)S(1)} %bitcast.25) | data formatting | bytes 3145728 | tf_op jit(solution)/shard_map/reshape | solution.py:451
  9.7 172.5 %prefix_attention.1 = (bf16[4,168,128]{2,1,0:T(8,128)(2,1)}, f32[8,1,128]{2,1,0:T(1,128)}) custom-call(s32[1]{0:T(128)S(6)} %copy.24.plen, bf16[4,168,128]{2,1,0:T(8,128)(2,1)} %bitcast.26, bf16[4,1536,128]{2,1,0:T(8,128)(2,1)} %bitcast.23, bf16[4,1536,128]{2,1,0:T(8,128)(2,1)} %bitcast.24, bf16[4,2,32,128]{3,2,1,0:T(8,128)(2,1)} %fusion.2.n_in, ...), custom_call_target="tpu_custom_call" | custom-call | tf_op jit(solution)/shard_map/prefix_attention/pallas_call | solution.py:462
  182.2 0.5 broadcast.64
  182.7 1.3 reduce.3
  184.1 0.1 reshape.67
  184.1 0.7 copy.18
  184.8 1.6 copy.25
  (2 shorter events, 0.0 us)
Async XLA Ops:
  3.9 2.9 %copy-start = (bf16[1536,4,128]{2,1,0:T(4,128)(2,1)S(1)}, bf16[1536,4,128]{2,1,0:T(4,128)(2,1)}, u32[]{:S(2)}) copy-start(bf16[1536,4,128]{2,1,0:T(4,128)(2,1)} %param.12) | copy-start | bytes 4718596
